TPU v7x, 32 devices: a whole 2x2x4 slice. The times are simulated.
32 devices in a mesh: gx: 4 (over x, core), gy: 4 (over z), gz: 2 (over y).
Axes of the slice: x: 2, y: 2, z: 4, core: 2. Of those that a mesh axis runs over, the one named last changes fastest.
Arguments:
- inv_factor: bfloat16 [4, 4, 2, 1536, 1536], P('gx', 'gy', 'gz'), as said below
- coupling: bfloat16 [4, 4, 2, 1536, 1536], P('gx', 'gy', 'gz'), may hold values from -0.15625 to 0.15625
- stiff_gg: bfloat16 [4, 4, 2, 1536, 1536], P('gx', 'gy', 'gz'), as said below
- block_order: int32 [4, 4, 2, 12], P('gx', 'gy', 'gz'), may hold values from 0 to 11, each once within a row
Outputs:
- assembled: float32 [4, 4, 2, 1536, 1536], P('gx', 'gy', 'gz')
Inputs may be any that keep to these rules, and one draw needn't show every extreme that they name: `block_order`: each subdomain's row is a permutation of 0 to 11. `stiff_gg`: each subdomain's block is symmetric. `inv_factor`: each subdomain's block is lower triangular with a positive diagonal.
All inputs are finite; a program needn't handle non-finite values.
Results may differ from a plain program's by a relative error of at most 0.0016.
Values sent between devices are 32-bit elements; how exact they have to be, the bound alone decides.
A program may use at most 128 MiB of HBM per device.

v0:
```python
import jax
import jax.numpy as jnp
from jax import lax
from jax.sharding import PartitionSpec as P

BLK = 128
NBLK = 12


west_blocks = (0,)
east_blocks = (1,)
south_blocks = (2, 8, 10)
north_blocks = (3, 9, 11)
bottom_blocks = (4, 5, 8, 9)
top_blocks = (6, 7, 10, 11)


def extended(array, sides, width):
    for axis, dim in sides:
        size, length = (lax.axis_size(axis), array.shape[dim])
        up = [(i, (i + 1) % size) for i in range(size - 1)]
        down = [(j, i) for i, j in up]
        last = lax.slice_in_dim(array, length - width, length, axis=dim)
        leading = lax.slice_in_dim(array, 0, width, axis=dim)
        before = lax.ppermute(last, axis, up)
        after = lax.ppermute(leading, axis, down)
        array = jnp.concatenate([before, array, after], axis=dim)
    return array


def pair_list(listed):
    count = len(listed)
    return [(first, second) for first in range(count) for second in range(count)]


def cut_piece(tile, row_block, col_block):
    return tile[row_block * BLK : (row_block + 1) * BLK, col_block * BLK : (col_block + 1) * BLK]


def add_piece(tile, row_block, col_block, piece):
    return tile.at[
        row_block * BLK : (row_block + 1) * BLK, col_block * BLK : (col_block + 1) * BLK
    ].add(piece)


def outgoing(tile, listed):
    return jnp.stack(
        [cut_piece(tile, listed[first], listed[second]) for first, second in pair_list(listed)]
    )


def absorb(tile, listed, received):
    for number, (first, second) in enumerate(pair_list(listed)):
        row_block = listed[first]
        col_block = listed[second]
        tile = add_piece(tile, row_block, col_block, received[number])
    return tile


def section_x(tile):
    message = jnp.stack([outgoing(tile, west_blocks), outgoing(tile, east_blocks)])
    padded = extended(message, (("gx", 0),), 1)
    tile = absorb(tile, west_blocks, padded[0])
    return absorb(tile, east_blocks, padded[3])


def section_y(tile):
    message = jnp.stack([outgoing(tile, south_blocks), outgoing(tile, north_blocks)])
    padded = extended(message, (("gy", 0),), 1)
    tile = absorb(tile, south_blocks, padded[0])
    return absorb(tile, north_blocks, padded[3])


def section_z(tile):
    message = jnp.stack([outgoing(tile, bottom_blocks), outgoing(tile, top_blocks)])
    padded = extended(message, (("gz", 0),), 1)
    tile = absorb(tile, bottom_blocks, padded[0])
    return absorb(tile, top_blocks, padded[3])


def shards(inv_factor, coupling, stiff_gg, block_order):
    ranking = block_order.reshape(NBLK)
    inverse = inv_factor[0, 0, 0]
    rows_inner = inverse.shape[0]
    coupled = coupling[0, 0, 0].reshape(rows_inner, NBLK, BLK)
    coupled = jnp.take(coupled, ranking, axis=1).reshape(rows_inner, NBLK * BLK)
    stiffness = stiff_gg[0, 0, 0].reshape(NBLK, BLK, NBLK, BLK)
    stiffness = jnp.take(jnp.take(stiffness, ranking, axis=0), ranking, axis=2).reshape(
        NBLK * BLK, NBLK * BLK
    )
    weighted = jnp.dot(inverse, coupled, preferred_element_type=jnp.float32).astype(jnp.bfloat16)
    product = lax.dot_general(
        weighted, weighted, (((0,), (0,)), ((), ())), preferred_element_type=jnp.float32
    )
    tile = stiffness.astype(jnp.float32) - product
    tile = section_x(tile)
    tile = section_z(section_y(tile))
    positions = jnp.arange(NBLK, dtype=jnp.int32)
    inverse_rank = jnp.sum(
        jnp.where(ranking[None, :] == positions[:, None], positions[None, :], 0), axis=1
    )
    blocked = tile.reshape(NBLK, BLK, NBLK, BLK)
    own = jnp.take(jnp.take(blocked, inverse_rank, axis=0), inverse_rank, axis=2)
    return own.reshape(1, 1, 1, NBLK * BLK, NBLK * BLK)


def solution(mesh):
    return jax.shard_map(
        shards,
        mesh=mesh,
        in_specs=(
            P("gx", "gy", "gz", None, None),
            P("gx", "gy", "gz", None, None),
            P("gx", "gy", "gz", None, None),
            P("gx", "gy", "gz", None),
        ),
        out_specs=P("gx", "gy", "gz", None, None),
        check_vma=False,
    )
```

profile of v0, /device:TPU:14, one launch (start us, length us, event | category | flops | bytes accessed | tf_op | source)
XLA Modules:
  0.0 332.4 jit_solution(16750717770328728103)
XLA Ops:
  2.1 9.4 %reshape_squeeze.6 = bf16[12,128,12,128]{3,2,1,0:T(8,128)(2,1)} reshape(bf16[1,1,1,1536,1536]{4,3,2,1,0:T(8,128)(2,1)} %param.110) | data formatting | bytes 9437184 | tf_op jit(solution)/shard_map/reshape;squeeze | solution.py:87
  11.5 6.3 %copy.17 = bf16[12,128,12,128]{3,1,2,0:T(8,128)(2,1)} copy(bf16[12,128,12,128]{3,2,1,0:T(8,128)(2,1)} %reshape_squeeze.6) | data formatting | bytes 9437184 | tf_op jit(solution)/shard_map/reshape;squeeze | solution.py:87
  17.9 5.8 %gather_fusion = bf16[12,128,12,128]{3,1,2,0:T(8,128)(2,1)} fusion(bf16[12,128,12,128]{3,1,2,0:T(8,128)(2,1)} %copy.17, s32[1024]{0:T(1024)S(1)} %get-tuple-element.680), kind=kCustom, calls=%fused_computation | custom fusion | bytes 9437232 | tf_op jit(solution)/shard_map/jit(_take)/gather | solution.py:88
  23.7 5.0 %broadcast_select_fusion.2 = bf16[12,128,12,128]{3,1,2,0:T(8,128)(2,1)} fusion(bf16[12,128,12,128]{3,1,2,0:T(8,128)(2,1)} %gather_fusion, pred[12]{0:T(512)(128)(4,1)S(1)} %compare_and_fusion), kind=kLoop, calls=%fused_computation.12 | loop fusion | flops 2359296 | bytes 9437196 | tf_op jit(solution)/shard_map/jit(_take)/select_n | solution.py:88
  28.8 5.8 %gather_fusion.1 = bf16[12,12,128,128]{3,2,1,0:T(8,128)(2,1)} fusion(bf16[12,128,12,128]{3,1,2,0:T(8,128)(2,1)} %broadcast_select_fusion.2, s32[1024]{0:T(1024)S(1)} %get-tuple-element.680), kind=kCustom, calls=%fused_computation.1 | custom fusion | bytes 9437232 | tf_op jit(solution)/shard_map/jit(_take)/gather | solution.py:88
  34.6 8.7 %copy.18 = bf16[12,128,12,128]{3,2,1,0:T(8,128)(2,1)} copy(bf16[12,128,12,128]{3,1,0,2:T(8,128)(2,1)} %bitcast.541) | data formatting | bytes 9437184 | tf_op jit(solution)/shard_map/jit(_take)/gather | solution.py:88
  43.3 6.6 %copy.19 = bf16[1,1,1,1536,1536]{3,4,2,1,0:T(8,128)(2,1)} copy(bf16[1,1,1,1536,1536]{4,3,2,1,0:T(8,128)(2,1)} %param.109) | data formatting | bytes 9437184 | tf_op args[1]
  49.9 6.6 %copy.20 = bf16[1536,12,128]{2,0,1:T(8,128)(2,1)} copy(bf16[1536,12,128]{0,2,1:T(8,128)(2,1)} %bitcast.542) | data formatting | bytes 9437184 | tf_op jit(solution)/shard_map/reshape;squeeze | solution.py:85
  56.5 5.8 %gather_fusion.2 = bf16[12,1536,128]{2,1,0:T(8,128)(2,1)} fusion(bf16[1536,12,128]{2,0,1:T(8,128)(2,1)} %copy.20, s32[1024]{0:T(1024)S(1)} %get-tuple-element.680), kind=kCustom, calls=%fused_computation.2 | custom fusion | bytes 9437232 | tf_op jit(solution)/shard_map/jit(_take)/gather | solution.py:86
  62.4 5.0 %select_bitcast_fusion = bf16[1536,12,128]{2,0,1:T(8,128)(2,1)} fusion(bf16[12,1536,128]{2,1,0:T(8,128)(2,1)} %gather_fusion.2, pred[12]{0:T(512)(128)(4,1)S(1)} %compare_and_fusion), kind=kLoop, calls=%fused_computation.9 | loop fusion | flops 2359296 | bytes 9437196 | tf_op jit(solution)/shard_map/jit(_take)/select_n | solution.py:86
  67.4 6.8 %copy.21 = bf16[1536,12,128]{0,2,1:T(8,128)(2,1)} copy(bf16[1536,12,128]{2,0,1:T(8,128)(2,1)} %select_bitcast_fusion) | data formatting | bytes 9437184 | tf_op jit(solution)/shard_map/jit(_take)/select_n | solution.py:86
  74.2 11.0 %convolution_convert_fusion = bf16[1536,1536]{1,0:T(8,128)(2,1)S(1)} fusion(bf16[1536,1536]{0,1:T(8,128)(2,1)} %bitcast.546, bf16[1,1,1,1536,1536]{4,3,2,1,0:T(8,128)(2,1)} %param.108), kind=kOutput, calls=%fused_computation.6 | convolution fusion | flops 7250116608 | bytes 14155776 | tf_op jit(solution)/shard_map/dot_general | solution.py:91
  85.2 11.5 %convert_subtract_fusion = f32[1536,1536]{1,0:T(8,128)} fusion(bf16[1536,1536]{1,0:T(8,128)(2,1)S(1)} %convolution_convert_fusion, bf16[192,8,12,128]{3,2,1,0:T(8,128)(2,1)S(1)} %bitcast.545, pred[1536]{0:T(1024)(128)(4,1)S(1)} %broadcast_bitcast_fusion), kind=kOutput, calls=%fused_computation.5 | convolution fusion | flops 7254835200 | bytes 18875904 | tf_op jit(solution)/shard_map/dot_general | solution.py:92
  123.8 10.7 %collective-permute-done.2 = f32[1,9,128,128]{3,2,1,0:T(8,128)S(1)} collective-permute-done((f32[1,9,128,128]{3,2,1,0:T(8,128)S(1)}, f32[1,9,128,128]{3,2,1,0:T(8,128)S(1)}, u32[]{:S(2)}, u32[]{:S(2)}) %collective-permute-start.2) | collective-permute-done | bytes 589856 | tf_op jit(solution)/shard_map/ppermute | solution.py:25
  176.8 4.7 %collective-permute-start.5 = (f32[1,16,128,128]{3,2,1,0:T(8,128)S(1)}, f32[1,16,128,128]{3,2,1,0:T(8,128)S(1)}, u32[]{:S(2)}, u32[]{:S(2)}) collective-permute-start(f32[1,16,128,128]{3,2,1,0:T(8,128)S(1)} %bitcast.549), channel_id=1, source_target_pairs={{1,0},{3,2},{5,4},{7,6},{9,8},{11,10},{13,12},{15,14},{17,16},{19,... | collective-permute-start | bytes 3145736 | tf_op jit(solution)/shard_map/ppermute | solution.py:26
  181.5 19.5 %collective-permute-done.4 = f32[1,16,128,128]{3,2,1,0:T(8,128)S(1)} collective-permute-done((f32[1,16,128,128]{3,2,1,0:T(8,128)S(1)}, f32[1,16,128,128]{3,2,1,0:T(8,128)S(1)}, u32[]{:S(2)}, u32[]{:S(2)}) %collective-permute-start.4) | collective-permute-done | bytes 1048608 | tf_op jit(solution)/shard_map/ppermute | solution.py:25
  248.4 11.6 %reshape.1905 = f32[12,128,12,128]{3,2,1,0:T(8,128)} reshape(f32[1536,1536]{1,0:T(8,128)} %fusion.2) | data formatting | bytes 18874368 | tf_op jit(solution)/shard_map/reshape | solution.py:102
  260.0 11.2 %copy.22 = f32[12,128,12,128]{3,1,2,0:T(8,128)} copy(f32[12,128,12,128]{3,2,1,0:T(8,128)} %reshape.1905) | data formatting | bytes 18874368 | tf_op jit(solution)/shard_map/reshape | solution.py:102
  271.1 8.5 %gather_fusion.3 = f32[12,128,12,128]{3,1,2,0:T(8,128)} fusion(f32[12,128,12,128]{3,1,2,0:T(8,128)} %copy.22, s32[1024]{0:T(1024)S(1)} %get-tuple-element.679), kind=kCustom, calls=%fused_computation.3 | custom fusion | bytes 18874416 | tf_op jit(solution)/shard_map/jit(_take)/gather | solution.py:103
  279.6 9.5 %broadcast_select_fusion.1 = f32[12,128,12,128]{3,1,2,0:T(8,128)} fusion(f32[12,128,12,128]{3,1,2,0:T(8,128)} %gather_fusion.3, pred[12]{0:T(512)(128)(4,1)S(1)} %compare_and_fusion.1), kind=kLoop, calls=%fused_computation.11 | loop fusion | flops 2359296 | bytes 18874380 | tf_op jit(solution)/shard_map/jit(_take)/select_n | solution.py:103
  289.1 8.4 %gather_fusion.4 = f32[12,12,128,128]{3,2,1,0:T(8,128)} fusion(f32[12,128,12,128]{3,1,2,0:T(8,128)} %broadcast_select_fusion.1, s32[1024]{0:T(1024)S(1)} %get-tuple-element.679), kind=kCustom, calls=%fused_computation.4 | custom fusion | bytes 18874416 | tf_op jit(solution)/shard_map/jit(_take)/gather | solution.py:103
  297.5 14.4 %copy.23 = f32[12,128,12,128]{3,2,1,0:T(8,128)} copy(f32[12,128,12,128]{3,1,0,2:T(8,128)} %bitcast.540) | data formatting | bytes 18874368 | tf_op jit(solution)/shard_map/jit(_take)/gather | solution.py:103
  311.9 11.9 %gather.30 = f32[1,1,1,1536,1536]{4,3,2,1,0:T(8,128)} reshape(f32[12,128,12,128]{3,2,1,0:T(8,128)} %copy.23) | data formatting | bytes 18874368 | tf_op jit(solution)/shard_map/jit(_take)/gather | solution.py:103
  323.8 8.6 %broadcast_select_fusion = f32[1,1,1,1536,1536]{4,3,2,1,0:T(8,128)} fusion(f32[1,1,1,1536,1536]{4,3,2,1,0:T(8,128)} %gather.30, pred[1536]{0:T(1024)(128)(4,1)S(1)} %broadcast_bitcast_fusion.1), kind=kLoop, calls=%fused_computation.10 | loop fusion | flops 2359296 | bytes 18875904 | tf_op jit(solution)/shard_map/jit(_take)/select_n | solution.py:103
  (102 shorter events, 118.7 us)
Async XLA Ops:
  67.4 17.8 %slice-start = ((s8[6291456]{0:T(1024)(128)(4,1)}), s8[2097152]{0:T(1024)(128)(4,1)S(1)}, s32[]{:S(2)}) async-start(s8[6291456]{0:T(1024)(128)(4,1)} %bitcast.543), calls=%async_computation | async-start | bytes 4194304
  74.2 11.0 %slice-start.1 = ((s8[6291456]{0:T(1024)(128)(4,1)}), s8[4194304]{0:T(1024)(128)(4,1)S(1)}, s32[]{:S(2)}) async-start(s8[6291456]{0:T(1024)(128)(4,1)} %bitcast.543), calls=%async_computation.1 | async-start | bytes 8388608
  97.6 5.6 %collective-permute-start = (f32[1,1,128,128]{3,2,1,0:T(8,128)S(1)}, f32[1,1,128,128]{3,2,1,0:T(8,128)S(1)}, u32[]{:S(2)}, u32[]{:S(2)}) collective-permute-start(f32[1,1,128,128]{3,2,1,0:T(8,128)S(1)} %slice_bitcast_fusion.97), channel_id=1, source_target_pairs={{0,8},{8,16},{16,24},{1,9},{9,17},{17,25},{2,10},{10,18},{18,26},{... | collective-permute-start | bytes 196616 | tf_op jit(solution)/shard_map/ppermute | solution.py:25
  104.7 3.8 %collective-permute-start.1 = (f32[1,1,128,128]{3,2,1,0:T(8,128)S(1)}, f32[1,1,128,128]{3,2,1,0:T(8,128)S(1)}, u32[]{:S(2)}, u32[]{:S(2)}) collective-permute-start(f32[1,1,128,128]{3,2,1,0:T(8,128)S(1)} %get-tuple-element.677), channel_id=1, source_target_pairs={{8,0},{16,8},{24,16},{9,1},{17,9},{25,17},{10,2},{18,10},{26,18},{... | collective-permute-start | bytes 196616 | tf_op jit(solution)/shard_map/ppermute | solution.py:26
  117.9 16.6 %collective-permute-start.2 = (f32[1,9,128,128]{3,2,1,0:T(8,128)S(1)}, f32[1,9,128,128]{3,2,1,0:T(8,128)S(1)}, u32[]{:S(2)}, u32[]{:S(2)}) collective-permute-start(f32[1,9,128,128]{3,2,1,0:T(8,128)S(1)} %bitcast.548), channel_id=1, source_target_pairs={{0,2},{2,4},{4,6},{1,3},{3,5},{5,7},{8,10},{10,12},{12,14},{9,11},... | collective-permute-start | bytes 1769480 | tf_op jit(solution)/shard_map/ppermute | solution.py:25
  121.4 26.5 %collective-permute-start.3 = (f32[1,9,128,128]{3,2,1,0:T(8,128)S(1)}, f32[1,9,128,128]{3,2,1,0:T(8,128)S(1)}, u32[]{:S(2)}, u32[]{:S(2)}) collective-permute-start(f32[1,9,128,128]{3,2,1,0:T(8,128)S(1)} %bitcast.547), channel_id=1, source_target_pairs={{2,0},{4,2},{6,4},{3,1},{5,3},{7,5},{10,8},{12,10},{14,12},{11,9},... | collective-permute-start | bytes 1769480 | tf_op jit(solution)/shard_map/ppermute | solution.py:26
  175.4 25.6 %collective-permute-start.4 = (f32[1,16,128,128]{3,2,1,0:T(8,128)S(1)}, f32[1,16,128,128]{3,2,1,0:T(8,128)S(1)}, u32[]{:S(2)}, u32[]{:S(2)}) collective-permute-start(f32[1,16,128,128]{3,2,1,0:T(8,128)S(1)} %bitcast.550), channel_id=1, source_target_pairs={{0,1},{2,3},{4,5},{6,7},{8,9},{10,11},{12,13},{14,15},{16,17},{18,... | collective-permute-start | bytes 3145736 | tf_op jit(solution)/shard_map/ppermute | solution.py:25
  176.8 47.9 %collective-permute-start.5 = (f32[1,16,128,128]{3,2,1,0:T(8,128)S(1)}, f32[1,16,128,128]{3,2,1,0:T(8,128)S(1)}, u32[]{:S(2)}, u32[]{:S(2)}) collective-permute-start(f32[1,16,128,128]{3,2,1,0:T(8,128)S(1)} %bitcast.549), channel_id=1, source_target_pairs={{1,0},{3,2},{5,4},{7,6},{9,8},{11,10},{13,12},{15,14},{17,16},{19,... | collective-permute-start | bytes 3145736 | tf_op jit(solution)/shard_map/ppermute | solution.py:26
where the time goes:
time: 338 us; the launch traced here: 332 us
  local copies, waits for them, and re-layouts  152 us (45%)
  other arithmetic  107 us (32%)
  waiting for transfers between devices  35.8 us (11%)
  matrix products  22.5 us (7%)
  starting transfers between devices  15.6 us (5%)
    scatter-add x50, other arithmetic, add_piece(): return tile.at[row_block * BLK:(row_block + 1) * BLK, col_block * BLK:(co...  74 us
    gather x3, local copies, waits for them, and re-layouts, shards(): jnp.take(jnp.take(blocked, inverse_rank, axis=0), inverse_rank, axis=2)  34.7 us
    ppermute x3, waiting for transfers between devices, extended(): before = lax.ppermute(last, axis, up)  33.9 us
    unnamed x28, local copies, waits for them, and re-layouts  27 us
    reshape x2, local copies, waits for them, and re-layouts, shards(): blocked = tile.reshape(NBLK, BLK, NBLK, BLK)  22.7 us
    another operation x2, local copies, waits for them, and re-layouts, shards(): stiffness = stiff_gg[0, 0, 0].reshape(NBLK, BLK, NBLK, BLK)  15.7 us
    gather x2, local copies, waits for them, and re-layouts, shards(): jnp.take(jnp.take(stiffness, ranking, axis=0), ranking, axis=2)  14.5 us
    dot_general x1, matrix products, shards(): lax.dot_general(weighted, weighted, (((0,), (0,)), ((), ())), preferred_e...  11.5 us
  transfers between devices with their start and end apart: 6, of which 4 were waited for; matrix products, arithmetic and copies ran while one was open for 11% of the time, Pallas kernels for 0%

commit v1 on v0

v1 whole, which is shorter than its diff:
```python
import functools

import jax
import jax.numpy as jnp
from jax import lax
from jax.experimental import pallas as pl
from jax.experimental.pallas import tpu as pltpu
from jax.sharding import PartitionSpec as P

HIGH_FIRST = (6, 7, 10, 11, 4, 5, 8, 9, 0, 1, 2, 3)
LOW_FIRST = (4, 5, 8, 9, 6, 7, 10, 11, 0, 1, 2, 3)
WEST, EAST = 8, 9
SOUTH, NORTH = (10, 2, 6), (11, 3, 7)
PANEL = 4
PANELS = 3
Z_PAIRS = ((0, 0), (0, 1), (0, 2), (0, 3), (1, 1), (1, 2), (1, 3), (2, 3), (2, 2), (3, 3))
Z_RUNS = ((0, 0, 4, 0), (1, 1, 3, 4), (2, 3, 1, 7), (2, 2, 1, 8), (3, 3, 1, 9))
Z_EARLY = 3
Y_PAIRS = ((1, 1), (2, 2), (0, 0), (0, 1), (0, 2), (1, 2))
MESH = pl.DeviceIdType.MESH


class Side:
    def __init__(self, axis):
        size = lax.axis_size(axis)
        self.axis = axis
        self.at = lax.axis_index(axis)
        self.lower = self.at > 0
        self.upper = self.at < size - 1
        self.size = size

    def toward(self, step):
        return {self.axis: self.at + step}


def slot_rank(order_ref, has_upper, slot):
    return jnp.where(has_upper, order_ref[HIGH_FIRST[slot]], order_ref[LOW_FIRST[slot]])


def weigh_part(inv_part, coupled, weighted, flipped, part):
    rows = inv_part.shape[0]
    here = pl.ds(part * rows, rows)
    product = jnp.dot(
        inv_part[...], coupled[pl.ds(0, (part + 1) * rows), :], preferred_element_type=jnp.float32
    ).astype(weighted.dtype)
    weighted[here, :] = product
    flipped[:, here] = product.T


def begin_kernel(
    order_ref, inv_hbm, coup_hbm, stiff_hbm,
    inv_0, inv_1, inv_2, coupled, stiff, weighted, flipped, tile, sems,
):
    inv_parts = (inv_0, inv_1, inv_2)
    parts = len(inv_parts)
    rows = inv_0.shape[0]
    slots, _, blk, _ = stiff.shape
    wide = PANEL * blk
    at = lax.axis_index("gz")
    has_upper = at < lax.axis_size("gz") - 1
    ranks = [slot_rank(order_ref, has_upper, slot) for slot in range(slots)]

    def span(slot):
        return pl.ds(pl.multiple_of(ranks[slot] * blk, blk), blk)

    def load_stiff(a, b, sem):
        pltpu.make_async_copy(stiff_hbm.at[span(a), span(b)], stiff.at[a, b], sem).start()

    for part in range(parts):
        here = pl.ds(part * rows, rows)
        for slot in range(PANEL):
            pltpu.make_async_copy(
                coup_hbm.at[here, span(slot)], coupled.at[here, pl.ds(slot * blk, blk)], sems.at[part]
            ).start()
        pltpu.make_async_copy(
            inv_hbm.at[here, pl.ds(0, (part + 1) * rows)], inv_parts[part], sems.at[parts + part]
        ).start()
    for a in range(PANEL):
        for b in range(PANEL):
            load_stiff(a, b, sems.at[2 * parts])
    for slot in range(PANEL, slots):
        pltpu.make_async_copy(
            coup_hbm.at[:, span(slot)], coupled.at[:, pl.ds(slot * blk, blk)], sems.at[2 * parts + 1]
        ).start()
    for a in range(PANEL):
        for b in range(PANEL, slots):
            load_stiff(a, b, sems.at[2 * parts + 2])
    for a in range(PANEL, slots):
        for b in range(slots):
            load_stiff(a, b, sems.at[2 * parts + 3])

    def arrived(ref, sem):
        pltpu.make_async_copy(ref, ref, sem).wait()

    panel = coupled.at[:, pl.ds(0, wide)]
    for part in range(parts):
        arrived(coupled.at[pl.ds(part * rows, rows), pl.ds(0, wide)], sems.at[part])
        arrived(inv_parts[part], sems.at[parts + part])
        weigh_part(inv_parts[part], panel, weighted, flipped, part)
    arrived(stiff.at[pl.ds(0, PANEL), pl.ds(0, PANEL)], sems.at[2 * parts])
    product = jnp.dot(flipped[...], weighted[...], preferred_element_type=jnp.float32)
    for a in range(PANEL):
        for b in range(PANEL):
            tile[a, b] = stiff[a, b].astype(jnp.float32) - product[
                a * blk : (a + 1) * blk, b * blk : (b + 1) * blk
            ]
    arrived(coupled.at[:, pl.ds(wide, (slots - PANEL) * blk)], sems.at[2 * parts + 1])
    arrived(stiff.at[pl.ds(0, PANEL), pl.ds(PANEL, slots - PANEL)], sems.at[2 * parts + 2])
    arrived(stiff.at[pl.ds(PANEL, slots - PANEL)], sems.at[2 * parts + 3])


def assemble_kernel(
    inv_0, inv_1, inv_2, coupled, stiff, weighted_0, flipped_0, tile_0, tile,
    weighted_1, weighted_2, flipped_1, flipped_2,
    got_x, got_y, got_z, x_send, x_recv, y_send, y_recv, z_send, z_recv,
):
    inv_parts = (inv_0, inv_1, inv_2)
    weighted = (weighted_0, weighted_1, weighted_2)
    flipped = (flipped_0, flipped_1, flipped_2)
    blk = tile.shape[-1]
    wide = PANEL * blk
    parts = len(inv_parts)
    gx, gy, gz = Side("gx"), Side("gy"), Side("gz")

    barrier = pltpu.get_barrier_semaphore()
    for side in (gx, gy, gz):
        @pl.when(side.lower)
        def _(side=side):
            pl.semaphore_signal(barrier, inc=1, device_id=side.toward(-1), device_id_type=MESH)

        @pl.when(side.upper)
        def _(side=side):
            pl.semaphore_signal(barrier, inc=1, device_id=side.toward(1), device_id_type=MESH)

    def weigh(panel, part):
        columns = coupled.at[:, pl.ds(panel * wide, wide)]
        weigh_part(inv_parts[part], columns, weighted[panel], flipped[panel], part)

    def multiply(first, second):
        product = jnp.dot(
            flipped[first][...], weighted[second][...], preferred_element_type=jnp.float32
        )
        for row in range(PANEL):
            for col in range(PANEL):
                a, b = first * PANEL + row, second * PANEL + col
                tile[a, b] = stiff[a, b].astype(jnp.float32) - product[
                    row * blk : (row + 1) * blk, col * blk : (col + 1) * blk
                ]

    def y_copy(number, up):
        mine, way = (NORTH, 1) if up else (SOUTH, 0)
        first, second = Y_PAIRS[number]
        return pltpu.make_async_remote_copy(
            src_ref=(tile_0 if number == 0 else tile).at[mine[first], mine[second]],
            dst_ref=got_y.at[1 - way, number],
            send_sem=y_send.at[way, number],
            recv_sem=y_recv.at[1 - way, number],
            device_id=gy.toward(1 if up else -1),
            device_id_type=MESH,
        )

    def y_arrival(number, from_lower):
        place = 0 if from_lower else 1
        return pltpu.make_async_remote_copy(
            src_ref=got_y.at[place, number],
            dst_ref=got_y.at[place, number],
            send_sem=y_send.at[1 - place, number],
            recv_sem=y_recv.at[place, number],
            device_id=gy.toward(-1 if from_lower else 1),
            device_id_type=MESH,
        )

    def y_start(numbers):
        @pl.when(gy.lower)
        def _():
            for number in numbers:
                y_copy(number, False).start()

        @pl.when(gy.upper)
        def _():
            for number in numbers:
                y_copy(number, True).start()

    def add_pair(a, b, value):
        tile[a, b] = tile[a, b] + value
        if a != b:
            tile[b, a] = tile[b, a] + value.T

    def y_finish(numbers):
        for has, mine, place, up in ((gy.lower, SOUTH, 0, False), (gy.upper, NORTH, 1, True)):
            @pl.when(has)
            def _(mine=mine, place=place, up=up):
                for number in numbers:
                    first, second = Y_PAIRS[number]
                    y_copy(number, up).wait_send()
                    y_arrival(number, place == 0).wait_recv()
                    add_pair(mine[first], mine[second], got_y[place, number])

    z_first = gz.lower | gz.upper
    z_both = gz.lower & gz.upper

    def z_copy(panel, run):
        row, col, count, place = Z_RUNS[run]
        if panel == 0:
            target = gz.at + jnp.where(gz.upper, 1, -1)
            kind = jnp.where(target < gz.size - 1, jnp.where(gz.upper, 1, 0), 0)
        else:
            target = gz.at - 1
            kind = 0
        return pltpu.make_async_remote_copy(
            src_ref=(tile_0 if panel == 0 and run < Z_EARLY else tile).at[
                panel * PANEL + row, pl.ds(panel * PANEL + col, count)
            ],
            dst_ref=got_z.at[kind, pl.ds(place, count)],
            send_sem=z_send.at[panel, run],
            recv_sem=z_recv.at[kind, run],
            device_id={"gz": target},
            device_id_type=MESH,
        )

    def z_start(panel, runs):
        @pl.when(z_first if panel == 0 else z_both)
        def _():
            for run in runs:
                z_copy(panel, run).start()

    def z_finish(panel):
        @pl.when(z_first if panel == 0 else z_both)
        def _():
            for run, (_, _, count, place) in enumerate(Z_RUNS):
                z_copy(panel, run).wait_send()
                pltpu.make_async_remote_copy(
                    src_ref=got_z.at[panel, pl.ds(place, count)],
                    dst_ref=got_z.at[panel, pl.ds(place, count)],
                    send_sem=z_send.at[panel, run],
                    recv_sem=z_recv.at[panel, run],
                    device_id={"gz": gz.at + (jnp.where(gz.upper, 1, -1) if panel == 0 else -1)},
                    device_id_type=MESH,
                ).wait_recv()
            for number, (row, col) in enumerate(Z_PAIRS):
                add_pair(panel * PANEL + row, panel * PANEL + col, got_z[panel, number])

    def x_copy(up):
        way, slot = (1, EAST) if up else (0, WEST)
        return pltpu.make_async_remote_copy(
            src_ref=tile.at[slot, slot],
            dst_ref=got_x.at[1 - way],
            send_sem=x_send.at[way],
            recv_sem=x_recv.at[1 - way],
            device_id=gx.toward(1 if up else -1),
            device_id_type=MESH,
        )

    def x_start():
        @pl.when(gx.lower)
        def _():
            x_copy(False).start()

        @pl.when(gx.upper)
        def _():
            x_copy(True).start()

    def x_finish():
        for has, slot, place, up in ((gx.lower, WEST, 0, False), (gx.upper, EAST, 1, True)):
            @pl.when(has)
            def _(slot=slot, place=place, up=up):
                x_copy(up).wait_send()
                pltpu.make_async_remote_copy(
                    src_ref=got_x.at[place],
                    dst_ref=got_x.at[place],
                    send_sem=x_send.at[1 - place],
                    recv_sem=x_recv.at[place],
                    device_id=gx.toward(1 if up else -1),
                    device_id_type=MESH,
                ).wait_recv()
                tile[slot, slot] = tile[slot, slot] + got_x[place]

    weigh(1, 0)
    neighbours = sum(
        side.lower.astype(jnp.int32) + side.upper.astype(jnp.int32) for side in (gx, gy, gz)
    )
    pl.semaphore_wait(barrier, neighbours)
    y_start((0,))
    z_start(0, range(Z_EARLY))
    tile[0:PANEL, 0:PANEL] = tile_0[...]
    for part in range(1, parts):
        weigh(1, part)
    multiply(1, 1)
    weigh(2, 0)
    y_start((1,))
    z_start(1, range(Z_EARLY))
    y_finish((0,))
    weigh(2, 1)
    z_start(0, range(Z_EARLY, len(Z_RUNS)))
    y_finish((1,))
    weigh(2, 2)
    z_start(1, range(Z_EARLY, len(Z_RUNS)))
    multiply(2, 2)
    multiply(2, 0)
    x_start()
    y_start((2, 3))
    multiply(2, 1)
    y_start((4,))
    multiply(0, 1)
    y_start((5,))
    multiply(1, 0)
    multiply(0, 2)
    multiply(1, 2)
    x_finish()
    y_finish((2, 3, 4, 5))
    z_finish(1)
    z_finish(0)


def place_kernel(order_ref, tile, out_hbm, sem):
    slots, _, blk, _ = tile.shape
    at = lax.axis_index("gz")
    has_upper = at < lax.axis_size("gz") - 1
    ranks = [slot_rank(order_ref, has_upper, slot) for slot in range(slots)]
    for a in range(slots):
        for b in range(slots):
            pltpu.make_async_copy(
                tile.at[a, b],
                out_hbm.at[
                    pl.ds(pl.multiple_of(ranks[a] * blk, blk), blk),
                    pl.ds(pl.multiple_of(ranks[b] * blk, blk), blk),
                ],
                sem,
            ).start()
    pltpu.make_async_copy(out_hbm, out_hbm, sem).wait()


def shards(inv_factor, coupling, stiff_gg, block_order):
    order = block_order.reshape(block_order.shape[-1:])
    inverse, coupled, stiffness = inv_factor[0, 0, 0], coupling[0, 0, 0], stiff_gg[0, 0, 0]
    slots = order.shape[0]
    inner, outer = coupled.shape
    blk = outer // slots
    parts = 3
    rows = inner // parts
    narrow = coupled.dtype
    smem = pl.BlockSpec(memory_space=pltpu.SMEM)
    vmem = pl.BlockSpec(memory_space=pltpu.VMEM)
    hbm = pl.BlockSpec(memory_space=pltpu.HBM)
    wide = PANEL * blk
    held = pl.pallas_call(
        begin_kernel,
        out_shape=[pltpu.VMEM((rows, (part + 1) * rows), narrow) for part in range(parts)]
        + [
            pltpu.VMEM((inner, outer), narrow),
            pltpu.VMEM((slots, slots, blk, blk), narrow),
            pltpu.VMEM((inner, wide), narrow),
            pltpu.VMEM((wide, inner), narrow),
            pltpu.VMEM((PANEL, PANEL, blk, blk), jnp.float32),
        ],
        in_specs=[smem, hbm, hbm, hbm],
        out_specs=[vmem] * (parts + 5),
        scratch_shapes=[pltpu.SemaphoreType.DMA((2 * parts + 4,))],
        compiler_params=pltpu.CompilerParams(vmem_limit_bytes=43 * 1024 * 1024),
        name="begin",
    )(order, inverse, coupled, stiffness)
    tile = pl.pallas_call(
        assemble_kernel,
        out_shape=pltpu.VMEM((slots, slots, blk, blk), jnp.float32),
        in_specs=[vmem] * (parts + 5),
        out_specs=vmem,
        scratch_shapes=[pltpu.VMEM((inner, wide), narrow)] * (PANELS - 1)
        + [pltpu.VMEM((wide, inner), narrow)] * (PANELS - 1)
        + [
            pltpu.VMEM((2, blk, blk), jnp.float32),
            pltpu.VMEM((2, len(Y_PAIRS), blk, blk), jnp.float32),
            pltpu.VMEM((2, len(Z_PAIRS), blk, blk), jnp.float32),
            pltpu.SemaphoreType.DMA((2,)),
            pltpu.SemaphoreType.DMA((2,)),
            pltpu.SemaphoreType.DMA((2, len(Y_PAIRS))),
            pltpu.SemaphoreType.DMA((2, len(Y_PAIRS))),
            pltpu.SemaphoreType.DMA((2, len(Z_RUNS))),
            pltpu.SemaphoreType.DMA((2, len(Z_RUNS))),
        ],
        compiler_params=pltpu.CompilerParams(
            collective_id=0, has_side_effects=True, vmem_limit_bytes=16 * 1024 * 1024
        ),
        name="assemble",
    )(*held)
    own = pl.pallas_call(
        place_kernel,
        out_shape=jax.ShapeDtypeStruct((outer, outer), jnp.float32),
        in_specs=[smem, pl.BlockSpec(memory_space=pl.ANY)],
        out_specs=hbm,
        scratch_shapes=[pltpu.SemaphoreType.DMA],
        compiler_params=pltpu.CompilerParams(vmem_limit_bytes=1024 * 1024),
        name="place",
    )(order, tile)
    return own.reshape(1, 1, 1, outer, outer)


def solution(mesh):
    return jax.shard_map(
        shards,
        mesh=mesh,
        in_specs=(
            P("gx", "gy", "gz", None, None),
            P("gx", "gy", "gz", None, None),
            P("gx", "gy", "gz", None, None),
            P("gx", "gy", "gz", None),
        ),
        out_specs=P("gx", "gy", "gz", None, None),
        check_vma=False,
    )
```

time: 338 us -> 30.6 us (0.09)
  the two profiles are of different devices: /device:TPU:14 before, /device:TPU:0 now
where the time goes in v1:
time: 30.6 us; the launch traced here: 30.5 us
  Pallas kernels  30.4 us (99%)
    pallas_call x1, Pallas kernels, shards(): pl.pallas_call(assemble_kernel, out_shape=pltpu.VMEM((slots, slots, blk,...  20.8 us
    pallas_call x1, Pallas kernels, shards(): pl.pallas_call(begin_kernel, out_shape=[pltpu.VMEM((rows, (part + 1) * ro...  5.58 us
    pallas_call x1, Pallas kernels, shards(): pl.pallas_call(place_kernel, out_shape=jax.ShapeDtypeStruct((outer, outer...  4.08 us

profile of v1, /device:TPU:0, one launch (start us, length us, event | category | flops | bytes accessed | tf_op | source)
XLA Modules:
  0.0 30.5 jit_solution(3887175399471523351)
XLA Ops:
  0.0 5.6 %begin.1 = (bf16[512,512]{1,0:T(8,128)(2,1)S(1)}, bf16[512,1024]{1,0:T(8,128)(2,1)S(1)}, bf16[512,1536]{1,0:T(8,128)(2,1)S(1)}, bf16[1536,1536]{1,0:T(8,128)(2,1...) custom-call(s32[12]{0:T(128)} %bitcast.5, ...), custom_call_target="tpu_custom_call" | custom-call | tf_op jit(solution)/shard_map/begin/pallas_call | solution.py:346
  5.6 0.0 copy-start
  5.6 20.8 %assemble.1.tile = f32[12,12,128,128]{3,2,1,0:T(8,128)S(1)} custom-call(bf16[512,512]{1,0:T(8,128)(2,1)S(1)} %get-tuple-element.13.inv_0, bf16[512,1024]{1,0:T(8,128)(2,1)S(1)} %get-tuple-element.14.inv_1, bf16[512,1536]{1,0:T(8,128)(2,1)S(1)} %get-tuple-element.15.inv_2, bf16[1536,1536]{1,0:T(8,128)(2,1)S(1)} %get-tuple-element.16.coupled, ...), custom_call_target="tpu_custom_call" | custom-call | tf_op jit(solution)/shard_map/assemble/pallas_call | solution.py:362
  26.4 0.0 copy-done
  26.4 4.1 %place.1 = f32[1536,1536]{1,0:T(8,128)} custom-call(s32[12]{0:T(128)S(1)} %bitcast.6, f32[12,12,128,128]{3,2,1,0:T(8,128)S(1)} %assemble.1.tile), custom_call_target="tpu_custom_call" | custom-call | tf_op jit(solution)/shard_map/place/pallas_call | solution.py:385
Async XLA Ops:
  5.6 20.8 %copy-start = (s32[1,1,1,12]{3,2,1,0:T(1,128)S(1)}, s32[1,1,1,12]{3,2,1,0:T(1,128)}, u32[]{:S(2)}) copy-start(s32[1,1,1,12]{3,2,1,0:T(1,128)} %param.7) | copy-start | bytes 148

commit v2 on v1

--- a/solution.py
+++ b/solution.py
@@ -275,7 +275,7 @@
                 ).wait_recv()
                 tile[slot, slot] = tile[slot, slot] + got_x[place]
 
-    weigh(1, 0)
+    weigh(2, 0)
     neighbours = sum(
         side.lower.astype(jnp.int32) + side.upper.astype(jnp.int32) for side in (gx, gy, gz)
     )
@@ -283,28 +283,28 @@
     y_start((0,))
     z_start(0, range(Z_EARLY))
     tile[0:PANEL, 0:PANEL] = tile_0[...]
-    for part in range(1, parts):
+    weigh(2, 1)
+    weigh(2, 2)
+    multiply(2, 2)
+    y_finish((0,))
+    x_start()
+    y_start((2,))
+    multiply(2, 0)
+    z_start(0, range(Z_EARLY, len(Z_RUNS)))
+    y_start((3,))
+    for part in range(parts):
         weigh(1, part)
     multiply(1, 1)
-    weigh(2, 0)
     y_start((1,))
     z_start(1, range(Z_EARLY))
-    y_finish((0,))
-    weigh(2, 1)
-    z_start(0, range(Z_EARLY, len(Z_RUNS)))
-    y_finish((1,))
-    weigh(2, 2)
-    z_start(1, range(Z_EARLY, len(Z_RUNS)))
-    multiply(2, 2)
-    multiply(2, 0)
-    x_start()
-    y_start((2, 3))
+    multiply(0, 1)
+    y_start((5,))
     multiply(2, 1)
     y_start((4,))
-    multiply(0, 1)
-    y_start((5,))
     multiply(1, 0)
+    y_finish((1,))
     multiply(0, 2)
+    z_start(1, range(Z_EARLY, len(Z_RUNS)))
     multiply(1, 2)
     x_finish()
     y_finish((2, 3, 4, 5))

time: 30.6 us -> 30 us (0.980)
  Pallas kernels: 30.4 us -> 29.8 us
    pallas_call x1, Pallas kernels: 20.8 us -> 20.2 us  [shards(): pl.pallas_call(assemble_kernel, out_shape=pltpu.VMEM((slots, slots, blk,...]
where the time goes in v2:
time: 30 us; the launch traced here: 29.9 us
  Pallas kernels  29.8 us (99%)
    pallas_call x1, Pallas kernels, shards(): pl.pallas_call(assemble_kernel, out_shape=pltpu.VMEM((slots, slots, blk,...  20.2 us
    pallas_call x1, Pallas kernels, shards(): pl.pallas_call(begin_kernel, out_shape=[pltpu.VMEM((rows, (part + 1) * ro...  5.58 us
    pallas_call x1, Pallas kernels, shards(): pl.pallas_call(place_kernel, out_shape=jax.ShapeDtypeStruct((outer, outer...  4.08 us

profile of v2, /device:TPU:0, one launch (start us, length us, event | category | flops | bytes accessed | tf_op | source)
XLA Modules:
  0.0 29.9 jit_solution(18433670690866171022)
XLA Ops:
  0.0 5.6 %begin.1 = (bf16[512,512]{1,0:T(8,128)(2,1)S(1)}, bf16[512,1024]{1,0:T(8,128)(2,1)S(1)}, bf16[512,1536]{1,0:T(8,128)(2,1)S(1)}, bf16[1536,1536]{1,0:T(8,128)(2,1...) custom-call(s32[12]{0:T(128)} %bitcast.5, ...), custom_call_target="tpu_custom_call" | custom-call | tf_op jit(solution)/shard_map/begin/pallas_call | solution.py:346
  5.6 0.0 copy-start
  5.6 20.2 %assemble.1.tile = f32[12,12,128,128]{3,2,1,0:T(8,128)S(1)} custom-call(bf16[512,512]{1,0:T(8,128)(2,1)S(1)} %get-tuple-element.13.inv_0, bf16[512,1024]{1,0:T(8,128)(2,1)S(1)} %get-tuple-element.14.inv_1, bf16[512,1536]{1,0:T(8,128)(2,1)S(1)} %get-tuple-element.15.inv_2, bf16[1536,1536]{1,0:T(8,128)(2,1)S(1)} %get-tuple-element.16.coupled, ...), custom_call_target="tpu_custom_call" | custom-call | tf_op jit(solution)/shard_map/assemble/pallas_call | solution.py:362
  25.8 0.0 copy-done
  25.8 4.1 %place.1 = f32[1536,1536]{1,0:T(8,128)} custom-call(s32[12]{0:T(128)S(1)} %bitcast.6, f32[12,12,128,128]{3,2,1,0:T(8,128)S(1)} %assemble.1.tile), custom_call_target="tpu_custom_call" | custom-call | tf_op jit(solution)/shard_map/place/pallas_call | solution.py:385
Async XLA Ops:
  5.6 20.2 %copy-start = (s32[1,1,1,12]{3,2,1,0:T(1,128)S(1)}, s32[1,1,1,12]{3,2,1,0:T(1,128)}, u32[]{:S(2)}) copy-start(s32[1,1,1,12]{3,2,1,0:T(1,128)} %param.7) | copy-start | bytes 148
